TPU v7x, 1024 devices: a whole 8x8x8 slice. The times are simulated.
1024 devices in a mesh: dom: 64 (over z, y), grp: 16 (over x, core).
Axes of the slice: x: 8, y: 8, z: 8, core: 2. Of those that a mesh axis runs over, the one named last changes fastest.
Arguments:
- old_state: float32 [9, 56, 131072], P(None, None, ('dom', 'grp')), may hold values from -6 to 6
- stiffness: float32 [3, 56, 56], replicated, may hold values from -0.75 to 0.75
- jacobians: float32 [3, 9, 9, 131072], P(None, None, None, ('dom', 'grp')), may hold values from -2 to 2
- lift_own: float32 [4, 56, 56], replicated, may hold values from -0.75 to 0.75
- lift_across: float32 [4, 4, 56, 56], replicated, may hold values from -0.75 to 0.75
- riemann: float32 [2, 4, 9, 9, 131072], P(None, None, None, None, ('dom', 'grp')), may hold values from -2 to 2
- cluster_ids: int32 [131072], P(('dom', 'grp')), may hold values from 0 to 2
- send_slots: int32 [327680], P(('dom', 'grp')), may hold values from 0 to 127, as said below
- face_partner: int32 [4, 131072], P(None, ('dom', 'grp')), may hold values from 0 to 447, as said below
- partner_face: int32 [4, 131072], P(None, ('dom', 'grp')), may hold values from 0 to 3
- cohesion: float32 [131072], P(('dom', 'grp')), may hold values from 1 to 4
- relax_time: float32 [131072], P(('dom', 'grp')), may hold values from 0.1 to 1
- yield_flag: int32 [131072], P(('dom', 'grp')), may hold values 0 or 1
Outputs:
- new_state: float32 [9, 56, 131072], P(None, None, ('dom', 'grp'))
Inputs may be any that keep to these rules, and one draw needn't show every extreme that they name: `send_slots`: local element numbers of the sending device; its first 256 slots go in equal shares to the devices of its grp group in grp order, the next 32 to the device one index lower along dom and the last 32 to the one one index higher, cyclically; the slots bound for one destination name distinct elements. `face_partner`: a place of the device's neighbour list: own elements, then what the grp group sends it, sender by sender, then what the lower and the higher dom neighbour send it; every received place is the partner of exactly one face of the device, all other faces have own places.
All inputs are finite; a program needn't handle non-finite values. No bound on the sum of `yield_flag` on one device may be relied on, other than what follows from the above.
Results may differ from a plain program's by a relative error of at most 0.0003.
Values sent between devices are 32-bit elements; how exact they have to be, the bound alone decides.
A program may use at most 64 MiB of HBM per device.

v0:
```python
import jax
import jax.numpy as jnp
from jax import lax
from jax.sharding import PartitionSpec as P

QUANT = 9
MODES = 56
ORDER = 6
GRP_SLOTS = 256
HALO = 32


base_step = 0.2
highest = lax.Precision.HIGHEST


def with_halo(shard, sides, width):
    for axis, dim in sides:
        count, length = (lax.axis_size(axis), shard.shape[dim])
        up = [(i, (i + 1) % count) for i in range(count)]
        down = [(j, i) for i, j in up]
        last = lax.slice_in_dim(shard, length - width, length, axis=dim)
        initial = lax.slice_in_dim(shard, 0, width, axis=dim)
        before = lax.ppermute(last, axis, up)
        after = lax.ppermute(initial, axis, down)
        shard = jnp.concatenate([before, shard, after], axis=dim)
    return shard


def step_table(terms_count):
    entries = []
    for rate_level in range(3):
        interval = base_step * 2.0**rate_level
        factorial = 1.0
        powers = []
        for degree in range(terms_count):
            factorial = factorial * (degree + 1)
            powers.append(interval ** (degree + 1) / factorial)
        entries.append(powers)
    return jnp.array(entries, dtype=jnp.float32)


def clock_steps():
    return jnp.array([base_step, 2.0 * base_step, 4.0 * base_step], dtype=jnp.float32)


def cluster_selector(cluster_ids):
    return (cluster_ids[None, :] == jnp.arange(3, dtype=jnp.int32)[:, None]).astype(jnp.float32)


def on_modes(matrix, operand):
    return jnp.einsum("mn,qne->qme", matrix, operand, precision=highest)


def on_quantities(operand, blocks):
    return jnp.sum(operand[:, None, :, :] * blocks[:, :, None, :], axis=0)


def taylor_stack(initial, stiffness, jacobian):
    collected = [initial]
    for degree in range(1, ORDER):
        latest = collected[-1]
        change = on_quantities(on_modes(stiffness[0], latest), jacobian[0])
        change = change + on_quantities(on_modes(stiffness[1], latest), jacobian[1])
        change = change + on_quantities(on_modes(stiffness[2], latest), jacobian[2])
        collected.append(-change)
    return jnp.stack(collected)


def integrate(stacked, weights):
    summed = weights[0] * stacked[0]
    for degree in range(1, stacked.shape[0]):
        summed = summed + weights[degree] * stacked[degree]
    return summed


def all_levels(collected, taylor_table):
    return jnp.stack(
        [integrate(collected, taylor_table[rate_level][:, None]) for rate_level in range(3)]
    )


def volume_term(own_int, stiffness, jacobian):
    summed = on_modes(stiffness[0].T, on_quantities(own_int, jacobian[0]))
    summed = summed + on_modes(stiffness[1].T, on_quantities(own_int, jacobian[1]))
    summed = summed + on_modes(stiffness[2].T, on_quantities(own_int, jacobian[2]))
    return summed


def face_update(own_int, neighbours, partner_sides, lift_own, lift_across, riemann):
    summed = jnp.zeros_like(own_int)
    candidates = jnp.arange(4, dtype=jnp.int32)[:, None]
    for face_index in range(4):
        summed = summed + on_quantities(
            on_modes(lift_own[face_index], own_int), riemann[0, face_index]
        )
        projected = jnp.einsum(
            "jmn,qne->qjme", lift_across[face_index], neighbours[face_index], precision=highest
        )
        picker = (partner_sides[face_index][None, :] == candidates).astype(jnp.float32)
        chosen = jnp.sum(projected * picker[None, :, None, :], axis=1)
        summed = summed + on_quantities(chosen, riemann[1, face_index])
    return summed


def plastic(updated, cohesion, relax_time, yielding, interval):
    isotropic = (jnp.arange(6, dtype=jnp.int32) < 3).astype(jnp.float32)[:, None, None]
    pressure = (updated[0] + updated[1] + updated[2]) / 3.0
    deviator = updated[:6] - isotropic * pressure[None]
    centre = deviator[:, 0, :]
    second = 0.5 * (centre[0] * centre[0] + centre[1] * centre[1] + centre[2] * centre[2])
    second = second + centre[3] * centre[3] + centre[4] * centre[4] + centre[5] * centre[5]
    strength = jnp.sqrt(second)
    excess = jnp.maximum(strength - cohesion, 0.0) / jnp.maximum(strength, cohesion)
    factor = yielding.astype(jnp.float32) * excess * (1.0 - jnp.exp(-interval / relax_time))
    return jnp.concatenate([updated[:6] - factor[None, None, :] * deviator, updated[6:]], axis=0)


def advance(
    own_block,
    stiffness,
    jacobian,
    lift_own,
    lift_across,
    riemann,
    selector,
    own_int,
    neighbours,
    partner_sides,
    cohesion,
    relax_time,
    yielding,
):
    updated = own_block + volume_term(own_int, stiffness, jacobian)
    updated = updated - face_update(
        own_int, neighbours, partner_sides, lift_own, lift_across, riemann
    )
    interval = jnp.sum(selector * clock_steps()[:, None], axis=0)
    return plastic(updated, cohesion, relax_time, yielding, interval)


def on_device(
    old_state,
    stiffness,
    jacobians,
    lift_own,
    lift_across,
    riemann,
    cluster_ids,
    send_slots,
    face_partner,
    partner_face,
    cohesion,
    relax_time,
    yield_flag,
):
    owned = old_state.shape[2]
    taylor_table = step_table(ORDER)
    selector = cluster_selector(cluster_ids)
    own_weights = jnp.sum(selector[:, None, :] * taylor_table[:, :, None], axis=0)
    collected = taylor_stack(old_state, stiffness, jacobians)
    own_int = integrate(collected, own_weights)
    payload = all_levels(collected, taylor_table).reshape(-1, owned)
    outgoing = jnp.take(payload, send_slots, axis=1)
    from_peers = lax.all_to_all(
        outgoing[:, :GRP_SLOTS], "grp", split_axis=1, concat_axis=1, tiled=True
    )
    padded = with_halo(outgoing[:, GRP_SLOTS:], (("dom", 1),), HALO)
    remote = jnp.concatenate([from_peers, padded[:, :HALO], padded[:, -HALO:]], axis=1)
    listing = jnp.concatenate([payload, remote], axis=1)
    neighbours = []
    for face_index in range(4):
        picked = jnp.take(listing, face_partner[face_index], axis=1)
        picked = picked.reshape(3, QUANT, MODES, owned)
        neighbours.append(jnp.sum(picked * selector[:, None, None, :], axis=0))
    return advance(
        old_state,
        stiffness,
        jacobians,
        lift_own,
        lift_across,
        riemann,
        selector,
        own_int,
        neighbours,
        partner_face,
        cohesion,
        relax_time,
        yield_flag,
    )


def solution(mesh):
    in_specs = (
        P(None, None, ("dom", "grp")),
        P(),
        P(None, None, None, ("dom", "grp")),
        P(),
        P(),
        P(None, None, None, None, ("dom", "grp")),
        P(("dom", "grp")),
        P(("dom", "grp")),
        P(None, ("dom", "grp")),
        P(None, ("dom", "grp")),
        P(("dom", "grp")),
        P(("dom", "grp")),
        P(("dom", "grp")),
    )
    out_specs = P(None, None, ("dom", "grp"))
    return jax.shard_map(
        on_device, mesh=mesh, in_specs=in_specs, out_specs=out_specs, check_vma=False
    )
```

profile of v0, /device:TPU:1, one launch (start us, length us, event | category | flops | bytes accessed | tf_op | source)
XLA Modules:
  0.0 104.1 jit_solution(4600351070556138640)
XLA Ops:
  0.0 1.3 %convolution_bitcast_fusion.20 = f32[9,56,128]{2,1,0:T(8,128)S(1)} fusion(f32[9,56,128]{2,1,0:T(8,128)} %param.17, f32[3,56,56]{2,1,0:T(8,128)} %param.18), kind=kOutput, calls=%fused_computation.66 | convolution fusion | flops 43352064 | bytes 544768 | tf_op jit(solution)/shard_map/mn,qne->qme/dot_general | solution.py:52
  1.4 1.4 %convolution_bitcast_fusion.21 = f32[9,56,128]{2,1,0:T(8,128)S(1)} fusion(f32[9,56,128]{2,1,0:T(8,128)} %param.17, f32[3,56,56]{2,1,0:T(8,128)} %param.18), kind=kOutput, calls=%fused_computation.67 | convolution fusion | flops 43352064 | bytes 544768 | tf_op jit(solution)/shard_map/mn,qne->qme/dot_general | solution.py:52
  2.8 1.4 %convolution_bitcast_fusion.22 = f32[9,56,128]{2,1,0:T(8,128)S(1)} fusion(f32[9,56,128]{2,1,0:T(8,128)} %param.17, f32[3,56,56]{2,1,0:T(8,128)} %param.18), kind=kOutput, calls=%fused_computation.68 | convolution fusion | flops 43352064 | bytes 544768 | tf_op jit(solution)/shard_map/mn,qne->qme/dot_general | solution.py:52
  4.1 1.2 %fusion.85 = (f32[1,9,9,128]{3,0,2,1:T(1,128)S(1)}, f32[1,9,9,128]{3,0,2,1:T(1,128)S(1)}, f32[1,9,9,128]{3,0,2,1:T(1,128)S(1)}) fusion(f32[3,9,9,128]{3,0,2,1:T(4,128)} %param.19), kind=kLoop, calls=%fused_computation.220 | loop fusion | bytes 248832 | tf_op jit(solution)/shard_map/slice | solution.py:64
  14.0 2.0 %gather_fusion = f32[320,1512]{1,0:T(8,128)S(1)} fusion(f32[1512,128]{0,1:T(8,128)S(1)} %copy.49, s32[1024]{0:T(1024)S(1)} %pad_clamp_fusion.4), kind=kCustom, calls=%fused_computation.4 | custom fusion | bytes 3872000 | tf_op jit(solution)/shard_map/jit(_take)/gather | solution.py:164
  16.2 1.3 %copy-done.2 = f32[1512,320]{0,1:T(8,128)} copy-done((f32[1512,320]{0,1:T(8,128)}, f32[1512,320]{0,1:T(8,128)S(1)}, u32[]{:S(2)}) %copy-start.2) | copy-done | bytes 1935384
  17.5 1.3 %slice.374 = f32[1512,256]{0,1:T(8,128)} slice(f32[1512,320]{0,1:T(8,128)S(1)} %select_bitcast_fusion), slice={[0:1512], [0:256]} | slice | bytes 3096576 | tf_op jit(solution)/shard_map/slice | solution.py:166
  18.8 17.7 %all-to-all-start = ((f32[1512,16,16]{0,2,1:T(8,128)}), f32[1512,16,16]{0,2,1:T(8,128)S(1)}, u32[]{:S(2)}, u32[]{:S(2)}) async-start(f32[1512,16,16]{0,2,1:T(8,128)} %bitcast.44), calls=%async_computation | async-start | bytes 3145728 | tf_op jit(solution)/shard_map/all_to_all | solution.py:165
  36.5 1.0 %fusion.83 = (f32[1512,32]{0,1:T(8,128)S(1)}, f32[1512,32]{0,1:T(8,128)S(1)}) fusion(f32[1512,320]{0,1:T(8,128)} %copy-done.2), kind=kLoop, calls=%fused_computation.218 | loop fusion | bytes 774144 | tf_op jit(solution)/shard_map/slice | solution.py:22
  37.6 1.9 %collective-permute-start = (f32[1512,32]{0,1:T(8,128)S(1)}, f32[1512,32]{0,1:T(8,128)S(1)}, u32[]{:S(2)}, u32[]{:S(2)}) collective-permute-start(f32[1512,32]{0,1:T(8,128)S(1)} %get-tuple-element.23), channel_id=1, source_target_pairs={{0,16},{16,32},{32,48},{48,64},{64,80},{80,96},{96,112},{112,128},... | collective-permute-start | bytes 580616 | tf_op jit(solution)/shard_map/ppermute | solution.py:24
  39.5 11.6 %collective-permute-start.1 = (f32[1512,32]{0,1:T(8,128)S(1)}, f32[1512,32]{0,1:T(8,128)}, u32[]{:S(2)}, u32[]{:S(2)}) collective-permute-start(f32[1512,32]{0,1:T(8,128)S(1)} %get-tuple-element.24), channel_id=1, source_target_pairs={{16,0},{32,16},{48,32},{64,48},{80,64},{96,80},{112,96},{128,112},... | collective-permute-start | bytes 580616 | tf_op jit(solution)/shard_map/ppermute | solution.py:25
  52.5 1.7 %fusion.84 = (f32[1,1,9,9,128]{4,1,3,2,0:T(1,128)S(1)}, f32[1,1,9,9,128]{4,1,3,2,0:T(1,128)S(1)}, f32[1,1,9,9,128]{4,1,3,2,0:T(1,128)S(1)}, f32[1,1,9,9,128]{4,1...) fusion(f32[2,4,9,9,128]{4,1,3,2,0:T(4,128)} %param.22), kind=kLoop, calls=%fused_computation.219 | loop fusion | bytes 663552 | tf_op jit(solution)/shard_map/slice | solution.py:102
  63.4 1.3 %multiply_reduce_fusion.8 = (f32[9,56,128]{2,1,0:T(8,128)}, f32[9,56,128]{2,1,0:T(8,128)S(1)}, f32[9,56,128]{2,1,0:T(8,128)S(1)}) fusion(f32[9,56,128]{2,1,0:T(8,128)S(1)} %get-tuple-element.27, f32[9,9,128]{2,1,0:T(8,128)S(1)} %get-tuple-element.55, f32[9,9,128]{2,1,0:T(8,128)S(1)} %get-tuple-element.56, f32[9,9,128]{2,1,0:T(8,128)S(1)} %bitcast.289), kind=kLoop, calls=%fused_computation.14 | loop fusion | flops 3290112 | bytes 1156608 | tf_op jit(solution)/shard_map/reduce_sum | solution.py:56
  65.1 1.1 %convolution_add_fusion.1 = f32[9,128,56]{1,2,0:T(8,128)} fusion(f32[9,128,56]{1,2,0:T(8,128)S(1)} %fusion.41, f32[9,56,128]{2,1,0:T(8,128)S(1)} %get-tuple-element.7, f32[3,56,56]{2,1,0:T(8,128)S(1)} %copy-done.7), kind=kOutput, calls=%fused_computation.49 | convolution fusion | flops 43416576 | bytes 802816 | tf_op jit(solution)/shard_map/mn,qne->qme/dot_general | solution.py:52
  67.5 7.6 %all-to-all-done = f32[1512,16,16]{0,2,1:T(8,128)S(1)} async-done(((f32[1512,16,16]{0,2,1:T(8,128)}), f32[1512,16,16]{0,2,1:T(8,128)S(1)}, u32[]{:S(2)}, u32[]{:S(2)}) %all-to-all-start) | async-done | bytes 1548320 | tf_op jit(solution)/shard_map/all_to_all | solution.py:165
  75.1 1.1 %copy-done.3 = f32[1512,16,16]{0,2,1:T(8,128)} copy-done((f32[1512,16,16]{0,2,1:T(8,128)}, f32[1512,16,16]{0,2,1:T(8,128)S(1)}, u32[]{:S(2)}) %copy-start.3) | copy-done | bytes 1548312
  76.3 1.8 %pad_maximum_fusion = f32[1512,448]{0,1:T(8,128)S(1)} fusion(f32[1512,32]{0,1:T(8,128)} %collective-permute-done.1, f32[1512,32]{0,1:T(8,128)} %copy-done.19, f32[1512,256]{0,1:T(8,128)} %bitcast.283, f32[1512,128]{0,1:T(8,128)S(1)} %copy.49), kind=kLoop, calls=%fused_computation.5 | loop fusion | flops 2032128 | bytes 5419008 | tf_op jit(solution)/shard_map/concatenate | solution.py:170
  78.1 1.9 %gather_fusion.2 = f32[128,1512]{1,0:T(8,128)} fusion(f32[1512,448]{0,1:T(8,128)S(1)} %pad_maximum_fusion, s32[1024]{0:T(1024)} %get-tuple-element.71), kind=kCustom, calls=%fused_computation.1.clone | custom fusion | bytes 1548800 | tf_op jit(solution)/shard_map/jit(_take)/gather | solution.py:173
  79.9 1.3 %select_bitcast_fusion.3 = f32[1512,128]{0,1:T(8,128)S(1)} fusion(f32[128,1512]{1,0:T(8,128)} %gather_fusion.2, pred[128]{0:T(512)(128)(4,1)} %get-tuple-element.49), kind=kLoop, calls=%fused_computation.71 | loop fusion | flops 193536 | bytes 1548416 | tf_op jit(solution)/shard_map/jit(_take)/select_n | solution.py:173
  81.2 1.1 %copy.53 = f32[1512,128]{1,0:T(8,128)} copy(f32[1512,128]{0,1:T(8,128)S(1)} %select_bitcast_fusion.3) | data formatting | bytes 1548288 | tf_op jit(solution)/shard_map/jit(_take)/select_n | solution.py:173
  82.3 1.9 %gather_fusion.3 = f32[128,1512]{1,0:T(8,128)} fusion(f32[1512,448]{0,1:T(8,128)S(1)} %pad_maximum_fusion, s32[1024]{0:T(1024)} %get-tuple-element.70), kind=kCustom, calls=%fused_computation.2.clone | custom fusion | bytes 1548800 | tf_op jit(solution)/shard_map/jit(_take)/gather | solution.py:173
  84.2 1.3 %select_bitcast_fusion.2 = f32[1512,128]{0,1:T(8,128)S(1)} fusion(f32[128,1512]{1,0:T(8,128)} %gather_fusion.3, pred[128]{0:T(512)(128)(4,1)} %get-tuple-element.53), kind=kLoop, calls=%fused_computation.70 | loop fusion | flops 193536 | bytes 1548416 | tf_op jit(solution)/shard_map/jit(_take)/select_n | solution.py:173
  85.5 1.2 %copy.56 = f32[1512,128]{1,0:T(8,128)} copy(f32[1512,128]{0,1:T(8,128)S(1)} %select_bitcast_fusion.2) | data formatting | bytes 1548288 | tf_op jit(solution)/shard_map/jit(_take)/select_n | solution.py:173
  86.6 1.9 %gather_fusion.4 = f32[128,1512]{1,0:T(8,128)} fusion(f32[1512,448]{0,1:T(8,128)S(1)} %pad_maximum_fusion, s32[1024]{0:T(1024)} %get-tuple-element.69), kind=kCustom, calls=%fused_computation.3.clone | custom fusion | bytes 1548800 | tf_op jit(solution)/shard_map/jit(_take)/gather | solution.py:173
  88.5 1.3 %select_bitcast_fusion.1 = f32[1512,128]{0,1:T(8,128)S(1)} fusion(f32[128,1512]{1,0:T(8,128)} %gather_fusion.4, pred[128]{0:T(512)(128)(4,1)} %get-tuple-element.13), kind=kLoop, calls=%fused_computation.69 | loop fusion | flops 193536 | bytes 1548416 | tf_op jit(solution)/shard_map/jit(_take)/select_n | solution.py:173
  89.8 1.2 %copy.59 = f32[1512,128]{1,0:T(8,128)} copy(f32[1512,128]{0,1:T(8,128)S(1)} %select_bitcast_fusion.1) | data formatting | bytes 1548288 | tf_op jit(solution)/shard_map/jit(_take)/select_n | solution.py:173
  90.9 1.9 %gather_fusion.1 = f32[128,1512]{1,0:T(8,128)} fusion(f32[1512,448]{0,1:T(8,128)S(1)} %pad_maximum_fusion, s32[1024]{0:T(1024)} %get-tuple-element.72), kind=kCustom, calls=%fused_computation.clone | custom fusion | bytes 1548800 | tf_op jit(solution)/shard_map/jit(_take)/gather | solution.py:173
  92.8 1.4 %select_bitcast_fusion.4 = f32[1512,128]{0,1:T(8,128)S(1)} fusion(f32[128,1512]{1,0:T(8,128)} %gather_fusion.1, pred[128]{0:T(512)(128)(4,1)} %get-tuple-element.51), kind=kLoop, calls=%fused_computation.72 | loop fusion | flops 193536 | bytes 1548416 | tf_op jit(solution)/shard_map/jit(_take)/select_n | solution.py:173
  94.2 1.1 %copy.50 = f32[1512,128]{1,0:T(8,128)} copy(f32[1512,128]{0,1:T(8,128)S(1)} %select_bitcast_fusion.4) | data formatting | bytes 1548288 | tf_op jit(solution)/shard_map/jit(_take)/select_n | solution.py:173
  95.4 1.6 %multiply_reduce_fusion.29 = (f32[9,56,128]{2,1,0:T(8,128)S(1)}, f32[9,56,128]{2,1,0:T(8,128)S(1)}, f32[9,56,128]{2,1,0:T(8,128)S(1)}, f32[9,56,128]{2,1,0:T(8,128)S(1)}) fusion(f32[3,9,56,128]{3,2,1,0:T(8,128)} %bitcast.293, f32[3,128]{1,0:T(4,128)S(1)} %fusion.70, f32[3,9,56,128]{3,2,1,0:T(8,128)S(1)} %bitcast.290, f32[3,9,56,128]{3,2,1,0:T(8,128)S(1)} %bitcast.291, ...), kind=kLoop, calls=%fused_computation.77 | loop fusion | flops 1290240 | bytes 4130304 | tf_op jit(solution)/shard_map/reduce_sum | solution.py:175
  97.1 1.0 fusion.5
  101.8 1.3 %fusion.10 = f32[9,56,128]{2,1,0:T(8,128)S(1)} fusion(f32[9,56,128]{2,1,0:T(8,128)S(1)} %copy-done.1, f32[9,128,56]{1,2,0:T(8,128)S(1)} %copy-done.13, f32[9,56,128]{2,1,0:T(8,128)S(1)} %copy-done.12, f32[9,56,128]{2,1,0:T(8,128)S(1)} %multiply_reduce_fusion, f32[9,56,128]{2,1,0:T(8,128)S(1)} %copy-done.8, f32[9,56,128]{2,1,0:T(8,128)S(1)} %multiply_reduce_fusion.2, ...), kind=kOutput, calls=%fused_computation.48 | convolution fusion | flops 43997184 | bytes 3125248 | tf_op jit(solution)/shard_map/mn,qne->qme/dot_general | solution.py:52
  (144 shorter events, 25.4 us)
Async XLA Ops:
  1.4 4.6 %copy-start.7 = (f32[3,56,56]{2,1,0:T(8,128)S(1)}, f32[3,56,56]{2,1,0:T(8,128)}, u32[]{:S(2)}) copy-start(f32[3,56,56]{2,1,0:T(8,128)} %param.18) | copy-start | bytes 112900
  10.7 1.8 %copy-start.22 = (s32[320]{0:T(512)S(1)}, s32[320]{0:T(512)}, u32[]{:S(2)}) copy-start(s32[320]{0:T(512)} %param.24) | copy-start | bytes 3844
  11.2 1.8 %copy-start.27 = (s32[128]{0:T(128)S(1)}, s32[128]{0:T(128)}, u32[]{:S(2)}) copy-start(s32[128]{0:T(128)} %param.23) | copy-start | bytes 1540
  11.2 1.9 %copy-start.26 = (f32[3,6]{1,0:T(4,128)S(1)}, f32[3,6]{1,0:T(4,128)}, u32[]{:S(2)}) copy-start(f32[3,6]{1,0:T(4,128)} %constant.43.clone) | copy-start | bytes 220
  11.2 1.9 %copy-start = (f32[9,56,128]{2,1,0:T(8,128)S(1)}, f32[9,56,128]{2,1,0:T(8,128)}, u32[]{:S(2)}) copy-start(f32[9,56,128]{2,1,0:T(8,128)} %param.17) | copy-start | bytes 774148
  18.8 32.3 %copy-start.20 = (f32[4,56,56]{2,1,0:T(8,128)S(1)}, f32[4,56,56]{2,1,0:T(8,128)}, u32[]{:S(2)}) copy-start(f32[4,56,56]{2,1,0:T(8,128)} %param.20) | copy-start | bytes 150532
  18.8 33.1 %copy-start.24 = (s32[4,128]{1,0:T(4,128)S(1)}, s32[4,128]{1,0:T(4,128)}, u32[]{:S(2)}) copy-start(s32[4,128]{1,0:T(4,128)} %param.25) | copy-start | bytes 6148
  18.8 35.4 %copy-start.32 = (f32[3]{0:T(128)S(1)}, f32[3]{0:T(128)}, u32[]{:S(2)}) copy-start(f32[3]{0:T(128)} %constant.44.clone) | copy-start | bytes 40
  18.8 56.3 %all-to-all-start = ((f32[1512,16,16]{0,2,1:T(8,128)}), f32[1512,16,16]{0,2,1:T(8,128)S(1)}, u32[]{:S(2)}, u32[]{:S(2)}) async-start(f32[1512,16,16]{0,2,1:T(8,128)} %bitcast.44), calls=%async_computation | async-start | bytes 3145728 | tf_op jit(solution)/shard_map/all_to_all | solution.py:165
  37.6 29.3 %collective-permute-start = (f32[1512,32]{0,1:T(8,128)S(1)}, f32[1512,32]{0,1:T(8,128)S(1)}, u32[]{:S(2)}, u32[]{:S(2)}) collective-permute-start(f32[1512,32]{0,1:T(8,128)S(1)} %get-tuple-element.23), channel_id=1, source_target_pairs={{0,16},{16,32},{32,48},{48,64},{64,80},{80,96},{96,112},{112,128},... | collective-permute-start | bytes 580616 | tf_op jit(solution)/shard_map/ppermute | solution.py:24
  39.5 28.0 %collective-permute-start.1 = (f32[1512,32]{0,1:T(8,128)S(1)}, f32[1512,32]{0,1:T(8,128)}, u32[]{:S(2)}, u32[]{:S(2)}) collective-permute-start(f32[1512,32]{0,1:T(8,128)S(1)} %get-tuple-element.24), channel_id=1, source_target_pairs={{16,0},{32,16},{48,32},{64,48},{80,64},{96,80},{112,96},{128,112},... | collective-permute-start | bytes 580616 | tf_op jit(solution)/shard_map/ppermute | solution.py:25
  58.8 5.9 %copy-start.25 = (s32[4,128]{1,0:T(4,128)S(1)}, s32[4,128]{1,0:T(4,128)}, u32[]{:S(2)}) copy-start(s32[4,128]{1,0:T(4,128)} %param.26) | copy-start | bytes 6148
  92.8 2.6 %copy-start.4 = (f32[1512,128]{1,0:T(8,128)S(1)}, f32[1512,128]{1,0:T(8,128)}, u32[]{:S(2)}) copy-start(f32[1512,128]{1,0:T(8,128)} %copy.53) | copy-start | bytes 2322436
  92.8 2.6 %copy-start.5 = (f32[1512,128]{1,0:T(8,128)S(1)}, f32[1512,128]{1,0:T(8,128)}, u32[]{:S(2)}) copy-start(f32[1512,128]{1,0:T(8,128)} %copy.56) | copy-start | bytes 2322436
  92.8 2.6 %copy-start.6 = (f32[1512,128]{1,0:T(8,128)S(1)}, f32[1512,128]{1,0:T(8,128)}, u32[]{:S(2)}) copy-start(f32[1512,128]{1,0:T(8,128)} %copy.59) | copy-start | bytes 2322436
  95.3 2.7 %copy-start.16 = (f32[9,9,128]{2,1,0:T(8,128)S(1)}, f32[9,9,128]{2,1,0:T(8,128)}, u32[]{:S(2)}) copy-start(f32[9,9,128]{2,1,0:T(8,128)} %get-tuple-element.59) | copy-start | bytes 124420
  95.4 2.9 %copy-start.21 = (f32[4,128]{1,0:T(4,128)S(1)}, f32[4,128]{1,0:T(4,128)}, u32[]{:S(2)}) copy-start(f32[4,128]{1,0:T(4,128)} %get-tuple-element.66) | copy-start | bytes 6148
  95.4 3.9 %copy-start.17 = (f32[9,9,128]{2,1,0:T(8,128)S(1)}, f32[9,9,128]{2,1,0:T(8,128)}, u32[]{:S(2)}) copy-start(f32[9,9,128]{2,1,0:T(8,128)} %get-tuple-element.61) | copy-start | bytes 124420
  97.0 3.4 %copy-start.18 = (f32[9,9,128]{2,1,0:T(8,128)S(1)}, f32[9,9,128]{2,1,0:T(8,128)}, u32[]{:S(2)}) copy-start(f32[9,9,128]{2,1,0:T(8,128)} %get-tuple-element.63) | copy-start | bytes 124420
  97.0 4.6 %copy-start.15 = (f32[9,9,128]{2,1,0:T(8,128)S(1)}, f32[9,9,128]{2,1,0:T(8,128)}, u32[]{:S(2)}) copy-start(f32[9,9,128]{2,1,0:T(8,128)} %get-tuple-element.57) | copy-start | bytes 124420
  97.0 4.8 %copy-start.1 = (f32[9,56,128]{2,1,0:T(8,128)S(1)}, f32[9,56,128]{2,1,0:T(8,128)}, u32[]{:S(2)}) copy-start(f32[9,56,128]{2,1,0:T(8,128)} %param.17) | copy-start | bytes 774148
  97.0 4.8 %copy-start.8 = (f32[9,56,128]{2,1,0:T(8,128)S(1)}, f32[9,56,128]{2,1,0:T(8,128)}, u32[]{:S(2)}) copy-start(f32[9,56,128]{2,1,0:T(8,128)} %multiply_reduce_fusion.1) | copy-start | bytes 774148
  97.0 4.8 %copy-start.9 = (f32[9,56,128]{2,1,0:T(8,128)S(1)}, f32[9,56,128]{2,1,0:T(8,128)}, u32[]{:S(2)}) copy-start(f32[9,56,128]{2,1,0:T(8,128)} %multiply_reduce_fusion.3) | copy-start | bytes 774148
  97.0 4.8 %copy-start.10 = (f32[9,56,128]{2,1,0:T(8,128)S(1)}, f32[9,56,128]{2,1,0:T(8,128)}, u32[]{:S(2)}) copy-start(f32[9,56,128]{2,1,0:T(8,128)} %multiply_reduce_fusion.5) | copy-start | bytes 774148
  97.1 4.8 %copy-start.11 = (f32[9,56,128]{2,1,0:T(8,128)S(1)}, f32[9,56,128]{2,1,0:T(8,128)}, u32[]{:S(2)}) copy-start(f32[9,56,128]{2,1,0:T(8,128)} %multiply_reduce_fusion.7) | copy-start | bytes 774148
  97.1 4.8 %copy-start.12 = (f32[9,56,128]{2,1,0:T(8,128)S(1)}, f32[9,56,128]{2,1,0:T(8,128)}, u32[]{:S(2)}) copy-start(f32[9,56,128]{2,1,0:T(8,128)} %get-tuple-element.6) | copy-start | bytes 774148
  97.1 4.7 %copy-start.13 = (f32[9,128,56]{1,2,0:T(8,128)S(1)}, f32[9,128,56]{1,2,0:T(8,128)}, u32[]{:S(2)}) copy-start(f32[9,128,56]{1,2,0:T(8,128)} %convolution_add_fusion.1) | copy-start | bytes 774148
  100.6 2.6 %copy-start.23 = (f32[6]{0:T(128)S(1)}, f32[6]{0:T(128)}, u32[]{:S(2)}) copy-start(f32[6]{0:T(128)} %compare_convert_fusion) | copy-start | bytes 76
  101.5 1.7 %copy-start.28 = (f32[128]{0:T(128)S(1)}, f32[128]{0:T(128)}, u32[]{:S(2)}) copy-start(f32[128]{0:T(128)} %param.28) | copy-start | bytes 1540
  101.5 1.7 %copy-start.29 = (f32[128]{0:T(128)S(1)}, f32[128]{0:T(128)}, u32[]{:S(2)}) copy-start(f32[128]{0:T(128)} %param.27) | copy-start | bytes 1540
  101.6 1.7 %copy-start.30 = (s32[128]{0:T(128)S(1)}, s32[128]{0:T(128)}, u32[]{:S(2)}) copy-start(s32[128]{0:T(128)} %param.29) | copy-start | bytes 1540
  101.6 1.7 %copy-start.31 = (f32[128]{0:T(128)S(1)}, f32[128]{0:T(128)}, u32[]{:S(2)}) copy-start(f32[128]{0:T(128)} %select_reduce_fusion) | copy-start | bytes 1540
  (4 other events, 4.8 us)
where the time goes:
time: 105 us; the launch traced here: 104 us
  starting transfers between devices  31.2 us (30%)
  local copies, waits for them, and re-layouts  25.4 us (24%)
  other arithmetic  22.1 us (21%)
  matrix products  17 us (16%)
  waiting for transfers between devices  7.61 us (7%)
    all_to_all x1, starting transfers between devices, on_device(): lax.all_to_all(outgoing[:, :GRP_SLOTS], 'grp', split_axis=1, concat_axis=...  17.7 us
    dot_general x22, matrix products, on_modes(): return jnp.einsum('mn,qne->qme', matrix, operand, precision=highest)  13.1 us
    ppermute x1, starting transfers between devices, with_halo(): after = lax.ppermute(initial, axis, down)  11.6 us
    reduce_sum x24, other arithmetic, on_quantities(): return jnp.sum(operand[:, None, :, :] * blocks[:, :, None, :], axis=0)  7.95 us
    all_to_all x1, waiting for transfers between devices, on_device(): lax.all_to_all(outgoing[:, :GRP_SLOTS], 'grp', split_axis=1, concat_axis=...  7.6 us
    gather x4, local copies, waits for them, and re-layouts, on_device(): picked = jnp.take(listing, face_partner[face_index], axis=1)  7.46 us
    select_n x4, other arithmetic, on_device(): picked = jnp.take(listing, face_partner[face_index], axis=1)  5.15 us
    select_n x4, local copies, waits for them, and re-layouts, on_device(): picked = jnp.take(listing, face_partner[face_index], axis=1)  4.6 us
  transfers between devices with their start and end apart: 3, of which 1 were waited for; matrix products, arithmetic and copies ran while one was open for 16% of the time, Pallas kernels for 0%

commit v1 on v0

v1 whole, which is shorter than its diff:
```python
import jax
import jax.numpy as jnp
from jax import lax
from jax.experimental import pallas as pl
from jax.experimental.pallas import tpu as pltpu
from jax.sharding import PartitionSpec as P

QUANT = 9
MODES = 56
ORDER = 6
ELEM = 128
GRP_SLOTS = 256
HALO = 32
N_GRP = 16
SHARE = GRP_SLOTS // N_GRP
CHIPS = N_GRP // 2
ROWS = QUANT * MODES
WIRE = 512
MESH = pl.DeviceIdType.MESH
F32 = jnp.float32
base_step = 0.2

PEERS = tuple(
    (d % CHIPS, c)
    for d in (4, 3, -3, 2, -2, 1, -1, 0)
    for c in (0, 1)
    if (d, c) != (0, 0)
)
N_PEERS = len(PEERS)
GROUPS = ((0, 32), (32, 24))


def taylor_table():
    entries = []
    for rate_level in range(3):
        interval = base_step * 2.0**rate_level
        factorial = 1.0
        powers = []
        for degree in range(ORDER):
            factorial = factorial * (degree + 1)
            powers.append(interval ** (degree + 1) / factorial)
        entries.append(powers)
    return entries


TABLE = taylor_table()


def split(x):
    hi = x.astype(jnp.bfloat16).astype(F32)
    return hi, x - hi


def dot(a, b):
    return lax.dot_general(a, b, (((1,), (0,)), ((), ())), preferred_element_type=F32)


def dot_nt(a, b):
    return lax.dot_general(a, b, (((1,), (1,)), ((), ())), preferred_element_type=F32)


def stack_weights(w, dst, rows):
    hi, lo = split(w)
    dst[rows, 0:128] = hi + pltpu.roll(hi, 64, 1)
    dst[rows, 128:256] = lo


def store_operand(rs, q, r0, rn, x):
    hi, lo = split(x)
    lanes = pl.ds(q * 128, 128)
    rs[pl.ds(r0, rn), lanes] = hi
    rs[pl.ds(64 + r0, rn), lanes] = lo
    rs[pl.ds(128 + r0, rn), lanes] = hi


def apply_modes(w, rs, kx, rows):
    for j in range(5):
        if j < 4:
            out = dot(w, rs[:, 256 * j : 256 * j + 256])
            kx[2 * j, 0:rows, :] = out[:, 0:128]
            kx[2 * j + 1, 0:rows, :] = out[:, 128:256]
        else:
            kx[8, 0:rows, :] = dot(w, rs[:, 1024:1152])


def kernel(
    old,
    stiff,
    jac,
    lown,
    lacross,
    riem,
    cluster,
    slots,
    fpart,
    pface,
    cohesion,
    relax_time,
    yflag,
    out,
    rs,
    kx,
    sb,
    wpad,
    wk,
    wown,
    wx,
    qm,
    lev,
    lv,
    near,
    upd,
    send,
    recv,
    rq_send,
    rq_recv,
    rq_ssem,
    rq_rsem,
    ssem,
    rsem,
):
    dom = lax.axis_index("dom")
    grp = lax.axis_index("grp")
    n_dom = lax.axis_size("dom")
    chip = grp // 2
    core = grp % 2
    below = ((dom + n_dom - 1) % n_dom, grp)
    above = ((dom + 1) % n_dom, grp)

    def peer(i):
        dx, dc = PEERS[i]
        return ((chip + dx) % CHIPS) * 2 + (core + dc) % 2

    def origin(i):
        dx, dc = PEERS[i]
        return ((chip + CHIPS - dx) % CHIPS) * 2 + (core + dc) % 2

    targets = [(dom, peer(i)) for i in range(N_PEERS)] + [below, above]

    barrier = pltpu.get_barrier_semaphore()
    for target in targets:
        pl.semaphore_signal(barrier, inc=1, device_id=target, device_id_type=MESH)

    for f in range(4):
        partner = fpart[pl.ds(f, 1), :]
        for c in range(4):
            place = lax.broadcasted_iota(jnp.int32, (128, 128), 0) + 128 * c
            qm[pl.ds(128 * c, 128), pl.ds(128 * f, 128)] = jnp.where(place == partner, 1.0, 0.0)

    ids = cluster[...]
    idsf = ids.astype(F32)
    ids4 = jnp.broadcast_to(jnp.concatenate([idsf] * 4, axis=1), (8, 512))
    wanted = dot_nt(ids4, qm[128:512, :])
    for t in range(3):
        rq_send[t] = wanted[0:1, 128 * t : 128 * t + 128]

    pl.semaphore_wait(barrier, N_PEERS + 2)

    requests = []
    for i in range(N_PEERS):
        requests.append(
            pltpu.make_async_remote_copy(
                src_ref=rq_send.at[peer(i) // 8],
                dst_ref=rq_recv.at[grp],
                send_sem=rq_ssem.at[i],
                recv_sem=rq_rsem.at[i],
                device_id=targets[i],
                device_id_type=MESH,
            )
        )
    for j in range(2):
        requests.append(
            pltpu.make_async_remote_copy(
                src_ref=rq_send.at[2],
                dst_ref=rq_recv.at[N_GRP + j],
                send_sem=rq_ssem.at[N_PEERS + j],
                recv_sem=rq_rsem.at[N_PEERS + j],
                device_id=targets[N_PEERS + j],
                device_id_type=MESH,
            )
        )
    for copy in requests:
        copy.start()
    rq_recv[grp] = rq_send[grp // 8]

    rs[...] = jnp.zeros_like(rs)
    wpad[...] = jnp.zeros_like(wpad)
    for d in range(3):
        wpad[d, 0:56, 0:56] = stiff[d]
    for d in range(3):
        w = wpad[d]
        stack_weights(w[0:56], wk, pl.ds(56 * d, 56))
        stack_weights(jnp.transpose(w)[0:56], wown, pl.ds(56 * d, 56))

    for d in range(3):
        for p in range(QUANT):
            for q in range(QUANT):
                sb[(d * 9 + p) * 9 + q] = jnp.broadcast_to(jac[d, p, pl.ds(q, 1), :], (8, 128))

    for q in range(QUANT):
        x = old[q]
        store_operand(rs, q, 0, 56, x)
        for c in range(3):
            lev[c, q] = x * F32(TABLE[c][0])

    def step(k, carry):
        apply_modes(wk[...], rs, kx, 168)
        coef = []
        for c in range(3):
            value = F32(TABLE[c][5])
            for j in range(1, 5):
                value = jnp.where(k == j, F32(TABLE[c][j]), value)
            coef.append(value)
        for r0, rn in GROUPS:
            acc = [None] * QUANT
            for d in range(3):
                for p in range(QUANT):
                    x = kx[p, 56 * d + r0 : 56 * d + r0 + rn, :].reshape(rn // 8, 8, 128)
                    for q in range(QUANT):
                        term = x * sb[(d * 9 + p) * 9 + q][None]
                        acc[q] = term if acc[q] is None else acc[q] + term
            for q in range(QUANT):
                x = -acc[q].reshape(rn, 128)
                store_operand(rs, q, r0, rn, x)
                for c in range(3):
                    lev[c, q, pl.ds(r0, rn), :] = lev[c, q, pl.ds(r0, rn), :] + coef[c] * x
        return carry

    lax.fori_loop(1, ORDER, step, 0)

    for c in range(3):
        for q in range(QUANT):
            hi, lo = split(lev[c, q])
            lv[c, 56 * q : 56 * q + 56, 0:128] = hi
            lv[c, 56 * q : 56 * q + 56, 128:256] = lo
        lv[c, ROWS:WIRE, :] = jnp.zeros((WIRE - ROWS, 256), F32)

    for i in range(N_PEERS + 2):
        requests[i].wait_recv()
    asked = rq_recv[...].reshape(N_GRP + 2, 128)
    lane = lax.broadcasted_iota(jnp.int32, (128, 256), 1)
    sub = lax.broadcasted_iota(jnp.int32, (128, 256), 0)
    pick = jnp.where(sub == SHARE * (grp % 8) + lane % SHARE, 1.0, 0.0)
    spread = dot(asked[0:N_GRP], pick)
    rows = lax.broadcasted_iota(jnp.int32, (N_GRP, 256), 0)
    cols = lax.broadcasted_iota(jnp.int32, (N_GRP, 256), 1)
    peer_level = jnp.sum(jnp.where(rows == cols // SHARE, spread, 0.0), axis=0, keepdims=True)
    halo_lane = lax.broadcasted_iota(jnp.int32, (1, 128), 1)
    from_above = asked[N_GRP : N_GRP + 1]
    from_below = asked[N_GRP + 1 : N_GRP + 2]
    halo_level = jnp.where(
        halo_lane < HALO,
        pltpu.roll(jnp.broadcast_to(from_below, (8, 128)), 128 - HALO, 1)[0:1],
        pltpu.roll(jnp.broadcast_to(from_above, (8, 128)), HALO, 1)[0:1],
    )
    level_row = jnp.concatenate([peer_level, halo_level], axis=1)
    slot_row = jnp.concatenate([slots[...].astype(F32), jnp.zeros((1, 64), F32)], axis=1)
    code = level_row * 128.0 + slot_row
    code = jnp.transpose(jnp.broadcast_to(code, (128, 384)))[0:320]
    lane_f = lax.broadcasted_iota(jnp.int32, (320, 128), 1).astype(F32)
    total = None
    for c in range(3):
        a = jnp.where(code == lane_f + 128.0 * c, 1.0, 0.0)
        part = dot_nt(jnp.concatenate([a, a], axis=1), lv[c])
        total = part if total is None else total + part
    send[...] = total

    copies = []
    for i in range(N_PEERS):
        copies.append(
            pltpu.make_async_remote_copy(
                src_ref=send.at[pl.ds(pl.multiple_of(peer(i) * SHARE, SHARE), SHARE)],
                dst_ref=recv.at[pl.ds(pl.multiple_of(grp * SHARE, SHARE), SHARE)],
                send_sem=ssem.at[i],
                recv_sem=rsem.at[i],
                device_id=targets[i],
                device_id_type=MESH,
            )
        )
    for j in range(2):
        copies.append(
            pltpu.make_async_remote_copy(
                src_ref=send.at[pl.ds(GRP_SLOTS + HALO * j, HALO)],
                dst_ref=recv.at[pl.ds(GRP_SLOTS + HALO * (1 - j), HALO)],
                send_sem=ssem.at[N_PEERS + j],
                recv_sem=rsem.at[N_PEERS + j],
                device_id=targets[N_PEERS + j],
                device_id_type=MESH,
            )
        )
    for copy in copies:
        copy.start()
    mine = pl.ds(pl.multiple_of(grp * SHARE, SHARE), SHARE)
    recv[mine, :] = send[mine, :]

    for q in range(QUANT):
        x = jnp.where(ids == 0, lev[0, q], jnp.where(ids == 1, lev[1, q], lev[2, q]))
        store_operand(rs, q, 0, 56, x)
    for f in range(4):
        wpad[0, 0:56, 0:56] = lown[f]
        stack_weights(wpad[0, 0:56, :], wown, pl.ds(168 + 56 * f, 56))
    apply_modes(wown[...], rs, kx, 392)
    for r0, rn in GROUPS:
        acc = [old[q, pl.ds(r0, rn), :].reshape(rn // 8, 8, 128) for q in range(QUANT)]
        for d in range(3):
            for p in range(QUANT):
                x = kx[p, 56 * d + r0 : 56 * d + r0 + rn, :].reshape(rn // 8, 8, 128)
                for q in range(QUANT):
                    acc[q] = acc[q] + x * sb[(d * 9 + p) * 9 + q][None]
        for f in range(4):
            for p in range(QUANT):
                x = kx[p, 168 + 56 * f + r0 : 168 + 56 * f + r0 + rn, :].reshape(rn // 8, 8, 128)
                for q in range(QUANT):
                    s = jnp.broadcast_to(riem[0, f, p, pl.ds(q, 1), :], (8, 128))
                    acc[q] = acc[q] - x * s[None]
        for q in range(QUANT):
            upd[q, pl.ds(r0, rn), :] = acc[q].reshape(rn, 128)

    for half in range(2):
        sel = qm[0:128, 256 * half : 256 * half + 256]
        ids2 = jnp.concatenate([ids, ids], axis=1)
        total = None
        for c in range(3):
            m = jnp.where(ids2 == c, sel, 0.0)
            part = dot(lv[c], jnp.concatenate([m, m], axis=0))
            total = part if total is None else total + part
        near[2 * half] = total[:, 0:128]
        near[2 * half + 1] = total[:, 128:256]

    for f in range(4):
        for j in range(4):
            wpad[0, 0:56, 0:56] = lacross[f, j]
            stack_weights(wpad[0, 0:56, :], wx.at[f], pl.ds(56 * j, 56))

    def add_received(first, count, row0):
        block = jnp.transpose(recv[first : first + 128, :])
        hi, lo = split(block)
        lhs = jnp.concatenate([hi, lo], axis=1)
        for half in range(2):
            m = qm[row0 : row0 + 128, 256 * half : 256 * half + 256]
            part = dot(lhs, jnp.concatenate([m, m], axis=0))
            near[2 * half] = near[2 * half] + part[:, 0:128]
            near[2 * half + 1] = near[2 * half + 1] + part[:, 128:256]

    recv[320:384, :] = jnp.zeros((64, WIRE), F32)
    for j in range(2):
        copies[N_PEERS + j].wait_recv()
    add_received(256, 64, 384)
    for i in range(N_PEERS):
        copies[i].wait_recv()
    add_received(0, 128, 128)
    add_received(128, 128, 256)

    for f in range(4):
        for q in range(QUANT):
            store_operand(rs, q, 0, 56, near[f, 56 * q : 56 * q + 56, :])
        apply_modes(wx[f], rs, kx, 224)
        side = pface[pl.ds(f, 1), :]
        is0 = side == 0
        is1 = side == 1
        is2 = side == 2
        for r0, rn in GROUPS:
            acc = [upd[q, pl.ds(r0, rn), :].reshape(rn // 8, 8, 128) for q in range(QUANT)]
            for p in range(QUANT):
                parts = [kx[p, 56 * j + r0 : 56 * j + r0 + rn, :] for j in range(4)]
                x = jnp.where(is0, parts[0], jnp.where(is1, parts[1], jnp.where(is2, parts[2], parts[3])))
                x = x.reshape(rn // 8, 8, 128)
                for q in range(QUANT):
                    s = jnp.broadcast_to(riem[1, f, p, pl.ds(q, 1), :], (8, 128))
                    acc[q] = acc[q] - x * s[None]
            for q in range(QUANT):
                upd[q, pl.ds(r0, rn), :] = acc[q].reshape(rn, 128)

    first = [upd[q, 0:1, :] for q in range(6)]
    mean = (first[0] + first[1] + first[2]) / 3.0
    dev = [first[q] - mean if q < 3 else first[q] for q in range(6)]
    second = 0.5 * (dev[0] * dev[0] + dev[1] * dev[1] + dev[2] * dev[2])
    second = second + dev[3] * dev[3] + dev[4] * dev[4] + dev[5] * dev[5]
    strength = jnp.sqrt(second)
    limit = cohesion[...]
    excess = jnp.maximum(strength - limit, 0.0) / jnp.maximum(strength, limit)
    interval = jnp.where(ids == 0, base_step, jnp.where(ids == 1, 2.0 * base_step, 4.0 * base_step))
    factor = yflag[...].astype(F32) * excess * (1.0 - jnp.exp(-interval / relax_time[...]))
    pressure = (upd[0] + upd[1] + upd[2]) / 3.0
    for q in range(QUANT):
        x = upd[q]
        if q < 3:
            out[q] = x - factor * (x - pressure)
        elif q < 6:
            out[q] = x - factor * x
        else:
            out[q] = x

    for copy in requests:
        copy.wait_send()
    for copy in copies:
        copy.wait_send()


def on_device(
    old_state,
    stiffness,
    jacobians,
    lift_own,
    lift_across,
    riemann,
    cluster_ids,
    send_slots,
    face_partner,
    partner_face,
    cohesion,
    relax_time,
    yield_flag,
):
    vmem = pl.BlockSpec(memory_space=pltpu.VMEM)
    args = (
        old_state,
        stiffness,
        jacobians,
        lift_own,
        lift_across,
        riemann,
        cluster_ids.reshape(1, ELEM),
        send_slots.reshape(1, 320),
        face_partner,
        partner_face,
        cohesion.reshape(1, ELEM),
        relax_time.reshape(1, ELEM),
        yield_flag.reshape(1, ELEM),
    )
    return pl.pallas_call(
        kernel,
        out_shape=jax.ShapeDtypeStruct((QUANT, MODES, ELEM), F32),
        in_specs=[vmem] * len(args),
        out_specs=vmem,
        scratch_shapes=[
            pltpu.VMEM((256, 1152), F32),
            pltpu.VMEM((QUANT, 392, 128), F32),
            pltpu.VMEM((243, 8, 128), F32),
            pltpu.VMEM((3, 128, 128), F32),
            pltpu.VMEM((168, 256), F32),
            pltpu.VMEM((392, 256), F32),
            pltpu.VMEM((4, 224, 256), F32),
            pltpu.VMEM((512, 512), F32),
            pltpu.VMEM((3, QUANT, MODES, 128), F32),
            pltpu.VMEM((3, WIRE, 256), F32),
            pltpu.VMEM((4, WIRE, 128), F32),
            pltpu.VMEM((QUANT, MODES, 128), F32),
            pltpu.VMEM((320, WIRE), F32),
            pltpu.VMEM((384, WIRE), F32),
            pltpu.VMEM((3, 1, 128), F32),
            pltpu.VMEM((N_GRP + 2, 1, 128), F32),
            pltpu.SemaphoreType.DMA((N_PEERS + 2,)),
            pltpu.SemaphoreType.DMA((N_PEERS + 2,)),
            pltpu.SemaphoreType.DMA((N_PEERS + 2,)),
            pltpu.SemaphoreType.DMA((N_PEERS + 2,)),
        ],
        compiler_params=pltpu.CompilerParams(
            collective_id=0, has_side_effects=True, vmem_limit_bytes=48 * 1024 * 1024
        ),
    )(*args)


def solution(mesh):
    in_specs = (
        P(None, None, ("dom", "grp")),
        P(),
        P(None, None, None, ("dom", "grp")),
        P(),
        P(),
        P(None, None, None, None, ("dom", "grp")),
        P(("dom", "grp")),
        P(("dom", "grp")),
        P(None, ("dom", "grp")),
        P(None, ("dom", "grp")),
        P(("dom", "grp")),
        P(("dom", "grp")),
        P(("dom", "grp")),
    )
    out_specs = P(None, None, ("dom", "grp"))
    return jax.shard_map(
        on_device, mesh=mesh, in_specs=in_specs, out_specs=out_specs, check_vma=False
    )
```

time: 105 us -> 47.8 us (0.46)
  Pallas kernels: 0 us -> 43.9 us
  starting transfers between devices: 31.2 us -> 0 us
  other arithmetic: 22.1 us -> 0 us
  local copies, waits for them, and re-layouts: 25.4 us -> 3.53 us
  matrix products: 17 us -> 0 us
  waiting for transfers between devices: 7.61 us -> 0 us
    pallas_call x0 -> x1, Pallas kernels: none -> 43.9 us  [on_device(): pl.pallas_call(kernel, out_shape=jax.ShapeDtypeStruct((QUANT, MODES, ELEM...]
    all_to_all x1 -> x0, starting transfers between devices: 17.7 us -> none  [on_device(): lax.all_to_all(outgoing[:, :GRP_SLOTS], 'grp', split_axis=1, concat_axis=...]
    dot_general x26 -> x0, matrix products: 17 us -> none  [the longest x22 13.1 us: on_modes(): return jnp.einsum('mn,qne->qme', matrix, operand, precision=highest)]
    ppermute x2 -> x0, starting transfers between devices: 13.5 us -> none  [the longest x1 11.6 us: with_halo(): after = lax.ppermute(initial, axis, down)]
    reduce_sum x27 -> x0, other arithmetic: 10.3 us -> none  [the longest x24 7.95 us: on_quantities(): return jnp.sum(operand[:, None, :, :] * blocks[:, :, None, :], axis=0)]
    gather x5 -> x0, local copies, waits for them, and re-layouts: 9.5 us -> none  [the longest x4 7.46 us: on_device(): picked = jnp.take(listing, face_partner[face_index], axis=1)]
    all_to_all x1 -> x0, waiting for transfers between devices: 7.6 us -> none  [on_device(): lax.all_to_all(outgoing[:, :GRP_SLOTS], 'grp', split_axis=1, concat_axis=...]
    select_n x6 -> x0, other arithmetic: 5.36 us -> none  [the longest x4 5.15 us: on_device(): picked = jnp.take(listing, face_partner[face_index], axis=1)]
  transfers between devices with their start and end apart: 3 -> 0, of which waited for: 1 -> 0; matrix products, arithmetic and copies ran while one was open for 16% -> 0% of each run, Pallas kernels for 0% -> 0%
where the time goes in v1:
time: 47.8 us; the launch traced here: 47.6 us
  Pallas kernels  43.9 us (92%)
  local copies, waits for them, and re-layouts  3.53 us (7%)
    pallas_call x1, Pallas kernels, on_device(): pl.pallas_call(kernel, out_shape=jax.ShapeDtypeStruct((QUANT, MODES, ELEM...  43.9 us
    unnamed x25, local copies, waits for them, and re-layouts  2.8 us

profile of v1, /device:TPU:1, one launch (start us, length us, event | category | flops | bytes accessed | tf_op | source)
XLA Modules:
  0.0 47.6 jit_solution(11611551458023677915)
XLA Ops:
  0.0 0.0 copy-start.10
  0.0 0.7 %reshape.16.slots = s32[1,320]{1,0:T(1,128)S(1)} reshape(s32[320]{0:T(512)} %param.20) | data formatting | bytes 2560 | tf_op jit(solution)/shard_map/reshape | solution.py:424
  0.7 0.0 copy-start.6
  0.7 0.0 copy-start.7
  0.7 0.0 copy-start.8
  0.7 0.0 copy-start.9
  0.7 1.0 %copy.14.jac = f32[3,9,9,128]{3,2,1,0:T(8,128)S(1)} copy(f32[3,9,9,128]{3,0,2,1:T(4,128)} %param.15) | data formatting | bytes 248832 | tf_op args[2]
  1.7 0.0 copy-done.10
  1.7 0.0 copy-start
  1.8 0.0 copy-start.1
  1.8 0.0 copy-start.2
  1.8 0.0 copy-start.3
  1.8 0.0 copy-start.4
  1.8 0.0 copy-start.5
  1.8 0.1 copy.15.riem
  1.9 0.0 copy-done.6
  1.9 0.0 copy-done.7
  1.9 0.0 copy-done.8
  1.9 0.0 copy-done.9
  1.9 0.8 %copy-done = f32[4,4,56,56]{3,2,1,0:T(8,128)S(1)} copy-done((f32[4,4,56,56]{3,2,1,0:T(8,128)S(1)}, f32[4,4,56,56]{3,2,1,0:T(8,128)}, u32[]{:S(2)}) %copy-start) | copy-done | bytes 200728
  2.8 0.1 copy-done.1
  2.8 0.1 copy-done.2
  2.9 0.0 copy-done.3
  2.9 0.0 copy-done.4
  2.9 0.0 copy-done.5
  2.9 43.9 %shard_map.127 = f32[9,56,128]{2,1,0:T(8,128)S(1)} custom-call(f32[9,56,128]{2,1,0:T(8,128)S(1)} %copy-done.1, f32[3,56,56]{2,1,0:T(8,128)S(1)} %copy-done.3, f32[3,9,9,128]{3,2,1,0:T(8,128)S(1)} %copy.14.jac, f32[4,56,56]{2,1,0:T(8,128)S(1)} %copy-done.2, f32[4,4,56,56]{3,2,1,0:T(8,128)S(1)} %copy-done, f32[2,4,9,9,128]{4,3,2,1,0:T(8,128)S(1)} %copy.15.riem, ...), custom_call_target="tpu_custom_call" | custom-call | tf_op jit(solution)/shard_map/pallas_call | solution.py:431
  46.9 0.7 %copy.17 = f32[9,56,128]{2,1,0:T(8,128)} copy(f32[9,56,128]{2,1,0:T(8,128)S(1)} %shard_map.127) | data formatting | bytes 516096
Async XLA Ops:
  0.0 1.7 %copy-start.10 = (f32[2,4,9,9,128]{4,1,3,2,0:T(4,128)S(1)}, f32[2,4,9,9,128]{4,1,3,2,0:T(4,128)}, u32[]{:S(2)}) copy-start(f32[2,4,9,9,128]{4,1,3,2,0:T(4,128)} %param.18) | copy-start | bytes 995332
  0.7 1.2 %copy-start.6 = (s32[128]{0:T(128)S(1)}, s32[128]{0:T(128)}, u32[]{:S(2)}) copy-start(s32[128]{0:T(128)} %param.19) | copy-start | bytes 1540
  0.7 1.2 %copy-start.7 = (f32[128]{0:T(128)S(1)}, f32[128]{0:T(128)}, u32[]{:S(2)}) copy-start(f32[128]{0:T(128)} %param.23) | copy-start | bytes 1540
  0.7 1.2 %copy-start.8 = (f32[128]{0:T(128)S(1)}, f32[128]{0:T(128)}, u32[]{:S(2)}) copy-start(f32[128]{0:T(128)} %param.24) | copy-start | bytes 1540
  0.7 1.2 %copy-start.9 = (s32[128]{0:T(128)S(1)}, s32[128]{0:T(128)}, u32[]{:S(2)}) copy-start(s32[128]{0:T(128)} %param.25) | copy-start | bytes 1540
  1.7 1.0 %copy-start = (f32[4,4,56,56]{3,2,1,0:T(8,128)S(1)}, f32[4,4,56,56]{3,2,1,0:T(8,128)}, u32[]{:S(2)}) copy-start(f32[4,4,56,56]{3,2,1,0:T(8,128)} %lacross.1) | copy-start | bytes 602116
  1.8 1.1 %copy-start.1 = (f32[9,56,128]{2,1,0:T(8,128)S(1)}, f32[9,56,128]{2,1,0:T(8,128)}, u32[]{:S(2)}) copy-start(f32[9,56,128]{2,1,0:T(8,128)} %old.1) | copy-start | bytes 774148
  1.8 1.1 %copy-start.2 = (f32[4,56,56]{2,1,0:T(8,128)S(1)}, f32[4,56,56]{2,1,0:T(8,128)}, u32[]{:S(2)}) copy-start(f32[4,56,56]{2,1,0:T(8,128)} %lown.1) | copy-start | bytes 150532
  1.8 1.2 %copy-start.3 = (f32[3,56,56]{2,1,0:T(8,128)S(1)}, f32[3,56,56]{2,1,0:T(8,128)}, u32[]{:S(2)}) copy-start(f32[3,56,56]{2,1,0:T(8,128)} %stiff.1) | copy-start | bytes 112900
  1.8 1.1 %copy-start.4 = (s32[4,128]{1,0:T(4,128)S(1)}, s32[4,128]{1,0:T(4,128)}, u32[]{:S(2)}) copy-start(s32[4,128]{1,0:T(4,128)} %fpart.1) | copy-start | bytes 6148
  1.8 1.1 %copy-start.5 = (s32[4,128]{1,0:T(4,128)S(1)}, s32[4,128]{1,0:T(4,128)}, u32[]{:S(2)}) copy-start(s32[4,128]{1,0:T(4,128)} %pface.1) | copy-start | bytes 6148

commit v2 on v1

v2 whole, which is shorter than its diff:
```python
import jax
import jax.numpy as jnp
from jax import lax
from jax.experimental import pallas as pl
from jax.experimental.pallas import tpu as pltpu
from jax.sharding import PartitionSpec as P

QUANT = 9
MODES = 56
ORDER = 6
ELEM = 128
GRP_SLOTS = 256
HALO = 32
N_GRP = 16
SHARE = GRP_SLOTS // N_GRP
CHIPS = N_GRP // 2
ROWS = QUANT * MODES
WIRE = 512
MESH = pl.DeviceIdType.MESH
F32 = jnp.float32
base_step = 0.2

PEERS = ((4, 0), (4, 1), (3, 0), (3, 1), (-3, 0), (-3, 1), (0, 1), (0, 0)) + (
    (2, 0), (2, 1), (-2, 0), (-2, 1), (1, 0), (1, 1), (-1, 0), (-1, 1))
SELF = 7
OTHERS = tuple(i for i in range(N_GRP) if i != SELF)
RAW = 2
EARLY = RAW * SHARE
RAW_WIRE = 768
ASKED = tuple(i for i in OTHERS if i >= RAW)
QGROUPS = ((0, 4), (4, 8), (8, 9))


def taylor_table():
    entries = []
    for rate_level in range(3):
        interval = base_step * 2.0**rate_level
        factorial = 1.0
        powers = []
        for degree in range(ORDER):
            factorial = factorial * (degree + 1)
            powers.append(interval ** (degree + 1) / factorial)
        entries.append(powers)
    return entries


TABLE = taylor_table()


def split(x):
    hi = x.astype(jnp.bfloat16).astype(F32)
    return hi, x - hi


def dot(a, b):
    return lax.dot_general(a, b, (((1,), (0,)), ((), ())), preferred_element_type=F32)


def dot_nt(a, b):
    return lax.dot_general(a, b, (((1,), (1,)), ((), ())), preferred_element_type=F32)


def stack_weights(w, dst, rows):
    hi, lo = split(w)
    dst[rows, 0:128] = hi + pltpu.roll(hi, 64, 1)
    dst[rows, 128:256] = lo


def store_operand(rs, q, x):
    hi, lo = split(x)
    lanes = pl.ds(q * 128, 128)
    rs[0:56, lanes] = hi
    rs[64:120, lanes] = lo
    rs[128:184, lanes] = hi


def apply_modes(w, rs, kx, rows, j):
    if j < 4:
        out = dot(w, rs[:, 256 * j : 256 * j + 256])
        kx[2 * j, 0:rows, :] = out[:, 0:128]
        kx[2 * j + 1, 0:rows, :] = out[:, 128:256]
    else:
        kx[8, 0:rows, :] = dot(w, rs[:, 1024:1152])


def tiles(x):
    return x.reshape(7, 8, 128)


def kernel(
    old_h,
    stiff_h,
    jac_h,
    lown_h,
    lacross_h,
    riem_h,
    cluster_h,
    slots_h,
    fpart_h,
    pface_h,
    cohesion_h,
    relax_h,
    yflag_h,
    out,
    old,
    stiff,
    jac,
    lown,
    lacross,
    riem,
    cluster,
    slots,
    fpart,
    pface,
    cohesion,
    relax_time,
    yflag,
    rs,
    kx,
    sb,
    wpad,
    wk,
    wown,
    wx,
    qm,
    lev,
    lv,
    sel,
    picked,
    near,
    chosen,
    upd,
    send,
    recv,
    raw,
    raw_send,
    raw_recv,
    raw_state,
    raw_sb,
    raw_near,
    rq_send,
    rq_recv,
    load_sem,
    rq_ssem,
    rq_rsem,
    ssem,
    rsem,
    met_sem,
):
    dom = lax.axis_index("dom")
    grp = lax.axis_index("grp")
    n_dom = lax.axis_size("dom")
    chip = grp // 2
    core = grp % 2
    below = ((dom + n_dom - 1) % n_dom, grp)
    above = ((dom + 1) % n_dom, grp)

    def peer(i):
        dx, dc = PEERS[i]
        return ((chip + dx + CHIPS) % CHIPS) * 2 + (core + dc) % 2

    def origin(i):
        dx, dc = PEERS[i]
        return ((chip - dx + CHIPS) % CHIPS) * 2 + (core + dc) % 2

    barrier = pltpu.get_barrier_semaphore()
    partner_core = (dom, chip * 2 + 1 - core)
    for i in OTHERS:
        if PEERS[i][1] == 0:

            @pl.when(core == 0)
            def _(i=i):
                pl.semaphore_signal(barrier, inc=1, device_id=(dom, peer(i)), device_id_type=MESH)

        else:

            @pl.when(core == 1)
            def _(i=i):
                pl.semaphore_signal(barrier, inc=1, device_id=(dom, peer(i)), device_id_type=MESH)

    for target in (below, above):
        pl.semaphore_signal(barrier, inc=1, device_id=(target[0], chip * 2 + 1), device_id_type=MESH)

    names = ("fpart", "cluster", "stiff", "old", "jac", "slots", "lown", "lacross", "riem", "pface", "coh", "relax", "flag")
    pairs = (
        (fpart_h, fpart), (cluster_h, cluster), (stiff_h, stiff), (old_h, old), (jac_h, jac), (slots_h, slots),
        (lown_h, lown), (lacross_h, lacross), (riem_h, riem), (pface_h, pface), (cohesion_h, cohesion),
        (relax_h, relax_time), (yflag_h, yflag),
    )
    loads = {}
    for n, (name, (src, dst)) in enumerate(zip(names, pairs)):
        loads[name] = pltpu.make_async_copy(src, dst, load_sem.at[n])
        loads[name].start()

    rs[...] = jnp.zeros_like(rs)
    wpad[...] = jnp.zeros_like(wpad)

    loads["fpart"].wait()
    loads["cluster"].wait()
    iota128 = lax.broadcasted_iota(jnp.int32, (128, 128), 0)
    iota16 = lax.broadcasted_iota(jnp.int32, (SHARE, 128), 0)
    for f in range(4):
        partner = fpart[pl.ds(f, 1), :]
        lanes = pl.ds(128 * f, 128)
        qm[0:128, lanes] = jnp.where(iota128 == partner, 1.0, 0.0)
        for i in range(N_GRP):
            moved = partner - (ELEM + SHARE * origin(i))
            qm[pl.ds(ELEM + SHARE * i, SHARE), lanes] = jnp.where(iota16 == moved, 1.0, 0.0)
        qm[384:512, lanes] = jnp.where(iota128 + 384 == partner, 1.0, 0.0)

    ids = cluster[...]
    idsf = ids.astype(F32)
    ids4 = jnp.broadcast_to(jnp.concatenate([idsf] * 4, axis=1), (8, 512))
    wanted = dot_nt(ids4, qm[128:512, :])
    for t in range(3):
        rq_send[t] = wanted[0:1, 128 * t : 128 * t + 128]
    rq_recv[SELF] = wanted[0:1, 0:128]
    for i in range(RAW):
        rq_recv[i] = jnp.zeros((1, 128), F32)

    loads["stiff"].wait()
    for d in range(3):
        wpad[d, 0:56, 0:56] = stiff[d]
    for d in range(3):
        w = wpad[d]
        stack_weights(-w[0:56], wk, pl.ds(56 * d, 56))
        stack_weights(jnp.transpose(w)[0:56], wown, pl.ds(56 * d, 56))
    loads["old"].wait()
    for q in range(QUANT):
        x = old[q]
        store_operand(rs.at[0], q, x)
        for c in range(3):
            lev[c, q] = x * F32(TABLE[c][0])
    loads["jac"].wait()
    for p in range(QUANT):
        for q in range(QUANT):
            for d in range(3):
                sb[(p * 9 + q) * 3 + d] = jnp.broadcast_to(jac[p, q, pl.ds(d, 1), :], (8, 128))

    for j in range(5):
        apply_modes(wk[...], rs.at[0], kx.at[0], 168, j)

    loads["slots"].wait()
    lane = lax.broadcasted_iota(jnp.int32, (1, 256), 1)
    place = lane % SHARE
    for i in range(N_GRP):
        place = place + jnp.where(lane // SHARE == i, SHARE * peer(i), 0)
    order = jnp.where(lax.broadcasted_iota(jnp.int32, (256, 256), 0) == place, 1.0, 0.0)
    slot_row = slots[...].astype(F32).reshape(1, 320)
    moved = dot(jnp.broadcast_to(slot_row[:, 0:256], (8, 256)), order)[0:1]
    slot_row = jnp.concatenate([moved, slot_row[:, 256:320], jnp.zeros((1, 64), F32)], axis=1)
    slot_col = jnp.transpose(jnp.broadcast_to(slot_row, (128, 384)))[0:320]
    lane_f = lax.broadcasted_iota(jnp.int32, (320, 128), 1).astype(F32)
    onehot = jnp.where(slot_col == lane_f, 1.0, 0.0)
    sel[:, 0:128] = onehot
    sel[:, 128:256] = onehot

    for q in range(QUANT):
        hi, lo = split(old[q])
        raw[56 * q : 56 * q + 56, 0:128] = hi
        raw[56 * q : 56 * q + 56, 128:256] = lo
    raw[ROWS:WIRE, :] = jnp.zeros((WIRE - ROWS, 256), F32)
    sub8 = lax.broadcasted_iota(jnp.int32, (8, 128), 0)
    for t in range(32):
        x = jnp.zeros((8, 128), F32)
        for i in range(8):
            if 8 * t + i < 243:
                x = jnp.where(sub8 == i, sb[8 * t + i], x)
        hi, lo = split(x)
        raw[WIRE + 8 * t : WIRE + 8 * t + 8, 0:128] = hi
        raw[WIRE + 8 * t : WIRE + 8 * t + 8, 128:256] = lo
    for n in range(3):
        raw_send[:, 256 * n : 256 * n + 256] = dot_nt(sel[0:EARLY, :], raw[256 * n : 256 * n + 256, :])
    raw_recv[EARLY:128, :] = jnp.zeros((128 - EARLY, RAW_WIRE), F32)

    def taylor_step(k, table, flip, take):
        src, dst = kx.at[(k - 1 + flip) % 2], kx.at[(k + flip) % 2]
        made = rs.at[(k + flip) % 2]
        for q0, q1 in QGROUPS:
            acc = {}
            for p in range(QUANT):
                for d in range(3):
                    x = tiles(src[p, 56 * d : 56 * d + 56, :])
                    for q in range(q0, q1):
                        term = x * table[(p * 9 + q) * 3 + d][None]
                        acc[q] = term if q not in acc else acc[q] + term
            for q in range(q0, q1):
                x = acc[q].reshape(56, 128)
                if k < ORDER - 1:
                    store_operand(made, q, x)
                take(k, q, x)
            if k < ORDER - 1:
                for j in range(q0 // 2, (q1 + 1) // 2):
                    apply_modes(wk[...], made, dst, 168, j)

    def take_levels(k, q, x):
        for c in range(3):
            total = lev[c, q] + F32(TABLE[c][k]) * x
            lev[c, q] = total
            if k == ORDER - 1:
                hi, lo = split(total)
                lv[c, 56 * q : 56 * q + 56, 0:128] = hi
                lv[c, 56 * q : 56 * q + 56, 128:256] = lo

    taylor_step(1, sb, 0, take_levels)

    @pl.when(core == 0)
    def _():
        pl.semaphore_wait(barrier, len(OTHERS))
        pl.semaphore_signal(met_sem.at[0], inc=1, device_id=partner_core, device_id_type=MESH)

    @pl.when(core == 1)
    def _():
        pl.semaphore_wait(met_sem.at[0], 1)

    requests = []
    for i in ASKED:
        requests.append(
            pltpu.make_async_remote_copy(
                src_ref=rq_send.at[i // 8],
                dst_ref=rq_recv.at[i],
                send_sem=rq_ssem.at[i],
                recv_sem=rq_rsem.at[i],
                device_id=(dom, origin(i)),
                device_id_type=MESH,
            )
        )
    for copy in requests:
        copy.start()
    copies = {}
    for i in range(RAW):
        copies[i] = pltpu.make_async_remote_copy(
            src_ref=raw_send.at[pl.ds(SHARE * i, SHARE)],
            dst_ref=raw_recv.at[pl.ds(SHARE * i, SHARE)],
            send_sem=ssem.at[i],
            recv_sem=rsem.at[i],
            device_id=(dom, peer(i)),
            device_id_type=MESH,
        )
        copies[i].start()
    loads["lown"].wait()

    for k in range(2, ORDER):
        taylor_step(k, sb, 0, take_levels)
    for c in range(3):
        lv[c, ROWS:WIRE, :] = jnp.zeros((WIRE - ROWS, 256), F32)
    for h in range(2):
        for c in range(3):
            picked[c, EARLY:320, 256 * h : 256 * h + 256] = dot_nt(
                sel[EARLY:320, :], lv[c, 256 * h : 256 * h + 256, :]
            )

    for copy in requests:
        copy.wait_recv()
    asked = rq_recv[0:N_GRP].reshape(N_GRP, 128)
    block = lax.broadcasted_iota(jnp.int32, (8, 128), 0)
    lane8 = lax.broadcasted_iota(jnp.int32, (8, 128), 1)
    rows = []
    for t in range(2):
        mine = jnp.where(block == lane8 // SHARE, asked[8 * t : 8 * t + 8], 0.0)
        rows.append(jnp.sum(mine, axis=0, keepdims=True))
    def fill(t, row, start, stop):
        span = pl.ds(128 * t + start, stop - start)
        col = jnp.transpose(jnp.broadcast_to(row, (128, 128)))[start:stop]
        is0 = col < 0.5
        is1 = col < 1.5
        for n in range(4):
            lanes = pl.ds(128 * n, 128)
            send[span, lanes] = jnp.where(
                is0, picked[0, span, lanes], jnp.where(is1, picked[1, span, lanes], picked[2, span, lanes])
            )

    fill(0, rows[0], EARLY, 128)
    fill(1, rows[1], 0, 128)

    for i in ASKED:
        copies[i] = pltpu.make_async_remote_copy(
            src_ref=send.at[pl.ds(SHARE * i, SHARE)],
            dst_ref=recv.at[pl.ds(SHARE * i, SHARE)],
            send_sem=ssem.at[i],
            recv_sem=rsem.at[i],
            device_id=(dom, peer(i)),
            device_id_type=MESH,
        )
    for i in copies:
        if i >= RAW:
            copies[i].start()
    recv[SHARE * SELF : SHARE * SELF + SHARE, :] = send[SHARE * SELF : SHARE * SELF + SHARE, :]

    for name in ("lacross", "riem", "pface", "coh", "relax"):
        loads[name].wait()

    @pl.when(core == 1)
    def _():
        pl.semaphore_wait(barrier, 4)
        pl.semaphore_signal(met_sem.at[1], inc=1, device_id=partner_core, device_id_type=MESH)

    @pl.when(core == 0)
    def _():
        pl.semaphore_wait(met_sem.at[1], 1)

    halo_requests = []
    for j, target in enumerate((below, above)):
        halo_requests.append(
            pltpu.make_async_remote_copy(
                src_ref=rq_send.at[2],
                dst_ref=rq_recv.at[N_GRP + j],
                send_sem=rq_ssem.at[N_GRP + j],
                recv_sem=rq_rsem.at[N_GRP + j],
                device_id=target,
                device_id_type=MESH,
            )
        )
    for copy in halo_requests:
        copy.start()
    loads["flag"].wait()

    for q in range(QUANT):
        x = jnp.where(ids == 0, lev[0, q], jnp.where(ids == 1, lev[1, q], lev[2, q]))
        store_operand(rs.at[0], q, x)
    for f in range(4):
        wpad[0, 0:56, 0:56] = lown[f]
        stack_weights(wpad[0, 0:56, :], wown, pl.ds(168 + 56 * f, 56))
    for j in range(5):
        apply_modes(wown[...], rs.at[0], kx.at[0], 392, j)

    def trace_terms(source, row0, side, f, acc, q0, q1):
        for p in range(QUANT):
            x = tiles(source[p, row0 : row0 + 56, :])
            for q in range(q0, q1):
                s = jnp.broadcast_to(riem[side, p, q, pl.ds(f, 1), :], (8, 128))
                acc[q] = acc[q] - x * s[None]

    for q0, q1 in QGROUPS:
        acc = {q: tiles(old[q]) for q in range(q0, q1)}
        for p in range(QUANT):
            for d in range(3):
                x = tiles(kx[0, p, 56 * d : 56 * d + 56, :])
                for q in range(q0, q1):
                    acc[q] = acc[q] + x * sb[(p * 9 + q) * 3 + d][None]
        for f in range(4):
            trace_terms(kx.at[0], 168 + 56 * f, 0, f, acc, q0, q1)
        for q in range(q0, q1):
            upd[q] = acc[q].reshape(56, 128)

    for copy in halo_requests:
        copy.wait_recv()
    from_above = jnp.broadcast_to(rq_recv[N_GRP], (8, 128))
    from_below = jnp.broadcast_to(rq_recv[N_GRP + 1], (8, 128))
    halo = jnp.where(
        lane8 < HALO, pltpu.roll(from_below, 128 - HALO, 1), pltpu.roll(from_above, HALO, 1)
    )
    fill(2, halo[0:1], 0, 64)
    for j, target in enumerate((below, above)):
        copies[N_GRP + j] = pltpu.make_async_remote_copy(
            src_ref=send.at[pl.ds(GRP_SLOTS + HALO * j, HALO)],
            dst_ref=recv.at[pl.ds(GRP_SLOTS + HALO * (1 - j), HALO)],
            send_sem=ssem.at[N_GRP + j],
            recv_sem=rsem.at[N_GRP + j],
            device_id=target,
            device_id_type=MESH,
        )
    for j in range(2):
        copies[N_GRP + j].start()
    for i in range(RAW):
        copies[i].wait_recv()

    ids2 = jnp.concatenate([ids, ids], axis=1)
    for half in range(2):
        m = qm[0:128, 256 * half : 256 * half + 256]
        total = None
        for c in range(3):
            mc = jnp.where(ids2 == c, m, 0.0)
            part = dot(lv[c], jnp.concatenate([mc, mc], axis=0))
            total = part if total is None else total + part
        near[2 * half] = total[:, 0:128]
        near[2 * half + 1] = total[:, 128:256]

    for f in range(4):
        for j in range(4):
            wpad[0, 0:56, 0:56] = lacross[f, j]
            stack_weights(wpad[0, 0:56, :], wx.at[f], pl.ds(56 * j, 56))

    raw_state[...] = jnp.transpose(raw_recv[...])
    for r in range(243):
        raw_sb[r] = jnp.broadcast_to(raw_state[pl.ds(WIRE + r, 1), :], (8, 128))
    level = rq_send[0]

    def weight(k):
        return jnp.where(level < 0.5, TABLE[0][k], jnp.where(level < 1.5, TABLE[1][k], TABLE[2][k]))

    def take_near(k, q, x):
        raw_near[56 * q : 56 * q + 56, :] = raw_near[56 * q : 56 * q + 56, :] + weight(k) * x

    for q in range(QUANT):
        x = raw_state[56 * q : 56 * q + 56, :]
        store_operand(rs.at[1], q, x)
        raw_near[56 * q : 56 * q + 56, :] = weight(0) * x
    raw_near[ROWS:WIRE, :] = jnp.zeros((WIRE - ROWS, 128), F32)
    for j in range(5):
        apply_modes(wk[...], rs.at[1], kx.at[1], 168, j)
    for k in range(1, ORDER):
        taylor_step(k, raw_sb, 1, take_near)

    def add_received(first, row0, extra):
        block = jnp.transpose(recv[first : first + 128, :])
        if extra is not None:
            block = block + extra
        hi, lo = split(block)
        lhs = jnp.concatenate([hi, lo], axis=1)
        for half in range(2):
            m = qm[row0 : row0 + 128, 256 * half : 256 * half + 256]
            part = dot(lhs, jnp.concatenate([m, m], axis=0))
            near[2 * half] = near[2 * half] + part[:, 0:128]
            near[2 * half + 1] = near[2 * half + 1] + part[:, 128:256]

    recv[320:384, :] = jnp.zeros((64, WIRE), F32)
    recv[0:EARLY, :] = jnp.zeros((EARLY, WIRE), F32)
    for j in range(2):
        copies[N_GRP + j].wait_recv()
    add_received(256, 384, None)
    for i in range(RAW, 8):
        if i != SELF:
            copies[i].wait_recv()
    add_received(0, 128, raw_near[...])
    for i in range(8, 16):
        copies[i].wait_recv()
    add_received(128, 256, None)

    for f in range(4):
        work = rs.at[f % 2]
        lifted = kx.at[f % 2]
        side = pface[pl.ds(f, 1), :]
        is0 = side == 0
        is1 = side == 1
        is2 = side == 2
        for q in range(QUANT):
            store_operand(work, q, near[f, 56 * q : 56 * q + 56, :])
        for j in range(5):
            apply_modes(wx[f], work, lifted, 224, j)
        for p in range(QUANT):
            parts = [lifted[p, 56 * j : 56 * j + 56, :] for j in range(4)]
            chosen[f % 2, p] = jnp.where(
                is0, parts[0], jnp.where(is1, parts[1], jnp.where(is2, parts[2], parts[3]))
            )
        for q0, q1 in QGROUPS:
            acc = {q: tiles(upd[q]) for q in range(q0, q1)}
            trace_terms(chosen.at[f % 2], 0, 1, f, acc, q0, q1)
            for q in range(q0, q1):
                upd[q] = acc[q].reshape(56, 128)

    first = [upd[q, 0:1, :] for q in range(6)]
    mean = (first[0] + first[1] + first[2]) / 3.0
    dev = [first[q] - mean if q < 3 else first[q] for q in range(6)]
    second = 0.5 * (dev[0] * dev[0] + dev[1] * dev[1] + dev[2] * dev[2])
    second = second + dev[3] * dev[3] + dev[4] * dev[4] + dev[5] * dev[5]
    strength = jnp.sqrt(second)
    limit = cohesion[...]
    excess = jnp.maximum(strength - limit, 0.0) / jnp.maximum(strength, limit)
    interval = jnp.where(ids == 0, base_step, jnp.where(ids == 1, 2.0 * base_step, 4.0 * base_step))
    factor = yflag[...].astype(F32) * excess * (1.0 - jnp.exp(-interval / relax_time[...]))
    pressure = (upd[0] + upd[1] + upd[2]) * F32(1.0 / 3.0)
    for q in range(QUANT):
        x = upd[q]
        if q < 3:
            out[q] = x - factor * (x - pressure)
        elif q < 6:
            out[q] = x - factor * x
        else:
            out[q] = x

    for copy in requests + halo_requests:
        copy.wait_send()
    for copy in copies.values():
        copy.wait_send()


def on_device(
    old_state,
    stiffness,
    jacobians,
    lift_own,
    lift_across,
    riemann,
    cluster_ids,
    send_slots,
    face_partner,
    partner_face,
    cohesion,
    relax_time,
    yield_flag,
):
    args = (
        old_state,
        stiffness,
        jnp.transpose(jacobians, (1, 2, 0, 3)),
        lift_own,
        lift_across,
        jnp.transpose(riemann, (0, 2, 3, 1, 4)),
        cluster_ids.reshape(1, ELEM),
        send_slots,
        face_partner,
        partner_face,
        cohesion.reshape(1, ELEM),
        relax_time.reshape(1, ELEM),
        yield_flag.reshape(1, ELEM),
    )
    args = tuple(pltpu.with_memory_space_constraint(a, pltpu.HBM) for a in args)
    sems = [pltpu.SemaphoreType.DMA((N_GRP + 2,)) for _ in range(4)]
    return pl.pallas_call(
        kernel,
        out_shape=jax.ShapeDtypeStruct((QUANT, MODES, ELEM), F32),
        in_specs=[pl.BlockSpec(memory_space=pltpu.HBM)] * len(args),
        out_specs=pl.BlockSpec(memory_space=pltpu.VMEM),
        scratch_shapes=[pltpu.VMEM(a.shape, a.dtype) for a in args]
        + [
            pltpu.VMEM((2, 256, 1152), F32),
            pltpu.VMEM((2, QUANT, 392, 128), F32),
            pltpu.VMEM((243, 8, 128), F32),
            pltpu.VMEM((3, 128, 128), F32),
            pltpu.VMEM((168, 256), F32),
            pltpu.VMEM((392, 256), F32),
            pltpu.VMEM((4, 224, 256), F32),
            pltpu.VMEM((512, 512), F32),
            pltpu.VMEM((3, QUANT, MODES, 128), F32),
            pltpu.VMEM((3, WIRE, 256), F32),
            pltpu.VMEM((320, 256), F32),
            pltpu.VMEM((3, 320, WIRE), F32),
            pltpu.VMEM((4, WIRE, 128), F32),
            pltpu.VMEM((2, QUANT, MODES, 128), F32),
            pltpu.VMEM((QUANT, MODES, 128), F32),
            pltpu.VMEM((320, WIRE), F32),
            pltpu.VMEM((384, WIRE), F32),
            pltpu.VMEM((RAW_WIRE, 256), F32),
            pltpu.VMEM((EARLY, RAW_WIRE), F32),
            pltpu.VMEM((128, RAW_WIRE), F32),
            pltpu.VMEM((RAW_WIRE, 128), F32),
            pltpu.VMEM((243, 8, 128), F32),
            pltpu.VMEM((WIRE, 128), F32),
            pltpu.VMEM((3, 1, 128), F32),
            pltpu.VMEM((N_GRP + 2, 1, 128), F32),
            pltpu.SemaphoreType.DMA((13,)),
        ]
        + sems
        + [pltpu.SemaphoreType.REGULAR((2,))],
        compiler_params=pltpu.CompilerParams(
            collective_id=0, has_side_effects=True, vmem_limit_bytes=40 * 1024 * 1024
        ),
    )(*args)


def solution(mesh):
    in_specs = (
        P(None, None, ("dom", "grp")),
        P(),
        P(None, None, None, ("dom", "grp")),
        P(),
        P(),
        P(None, None, None, None, ("dom", "grp")),
        P(("dom", "grp")),
        P(("dom", "grp")),
        P(None, ("dom", "grp")),
        P(None, ("dom", "grp")),
        P(("dom", "grp")),
        P(("dom", "grp")),
        P(("dom", "grp")),
    )
    out_specs = P(None, None, ("dom", "grp"))
    return jax.shard_map(
        on_device, mesh=mesh, in_specs=in_specs, out_specs=out_specs, check_vma=False
    )
```

time: 47.8 us -> 40.6 us (0.85)
  Pallas kernels: 43.9 us -> 39.7 us
  local copies, waits for them, and re-layouts: 3.53 us -> 0.7 us
    pallas_call x1, Pallas kernels: 43.9 us -> 39.7 us  [on_device(): pl.pallas_call(kernel, out_shape=jax.ShapeDtypeStruct((QUANT, MODES, ELEM...]
    unnamed x25 -> x1, local copies, waits for them, and re-layouts: 2.8 us -> 0.7 us
    reshape x1 -> x0, local copies, waits for them, and re-layouts: 0.73 us -> none  [on_device(): send_slots.reshape(1, 320)]
where the time goes in v2:
time: 40.6 us; the launch traced here: 40.4 us
  Pallas kernels  39.7 us (98%)
  local copies, waits for them, and re-layouts  0.7 us (2%)
    pallas_call x1, Pallas kernels, on_device(): pl.pallas_call(kernel, out_shape=jax.ShapeDtypeStruct((QUANT, MODES, ELEM...  39.7 us

profile of v2, /device:TPU:1, one launch (start us, length us, event | category | flops | bytes accessed | tf_op | source)
XLA Modules:
  0.0 40.4 jit_solution(2815355735055281527)
XLA Ops:
  0.0 39.7 %shard_map.127 = f32[9,56,128]{2,1,0:T(8,128)S(1)} custom-call(f32[9,56,128]{2,1,0:T(8,128)} %old_h.1, f32[3,56,56]{2,1,0:T(8,128)} %stiff_h.1, f32[9,9,3,128]{3,2,1,0:T(4,128)} %bitcast.7, f32[4,56,56]{2,1,0:T(8,128)} %lown_h.1, f32[4,4,56,56]{3,2,1,0:T(8,128)} %lacross_h.1, f32[2,9,9,4,128]{4,3,2,1,0:T(4,128)} %bitcast.6, s32[1,128]{1,0:T(1,128)} %bitcast.8, ...), custom_call_target="tpu_custom_call" | custom-call | tf_op jit(solution)/shard_map/pallas_call | solution.py:610
  39.7 0.7 %copy.15 = f32[9,56,128]{2,1,0:T(8,128)} copy(f32[9,56,128]{2,1,0:T(8,128)S(1)} %shard_map.127) | data formatting | bytes 516096

commit v3 on v2

--- a/solution.py
+++ b/solution.py
@@ -340,8 +340,35 @@
         copies[i].start()
     loads["lown"].wait()
 
-    for k in range(2, ORDER):
+    for k in range(2, ORDER - 1):
         taylor_step(k, sb, 0, take_levels)
+
+    @pl.when(core == 1)
+    def _():
+        pl.semaphore_wait(barrier, 4)
+        pl.semaphore_signal(met_sem.at[1], inc=1, device_id=partner_core, device_id_type=MESH)
+
+    @pl.when(core == 0)
+    def _():
+        pl.semaphore_wait(met_sem.at[1], 1)
+
+    halo_requests = []
+    for j, target in enumerate((below, above)):
+        halo_requests.append(
+            pltpu.make_async_remote_copy(
+                src_ref=rq_send.at[2],
+                dst_ref=rq_recv.at[N_GRP + j],
+                send_sem=rq_ssem.at[N_GRP + j],
+                recv_sem=rq_rsem.at[N_GRP + j],
+                device_id=target,
+                device_id_type=MESH,
+            )
+        )
+    for copy in halo_requests:
+        copy.start()
+    loads["flag"].wait()
+
+    taylor_step(ORDER - 1, sb, 0, take_levels)
     for c in range(3):
         lv[c, ROWS:WIRE, :] = jnp.zeros((WIRE - ROWS, 256), F32)
     for h in range(2):
@@ -389,31 +416,6 @@
 
     for name in ("lacross", "riem", "pface", "coh", "relax"):
         loads[name].wait()
-
-    @pl.when(core == 1)
-    def _():
-        pl.semaphore_wait(barrier, 4)
-        pl.semaphore_signal(met_sem.at[1], inc=1, device_id=partner_core, device_id_type=MESH)
-
-    @pl.when(core == 0)
-    def _():
-        pl.semaphore_wait(met_sem.at[1], 1)
-
-    halo_requests = []
-    for j, target in enumerate((below, above)):
-        halo_requests.append(
-            pltpu.make_async_remote_copy(
-                src_ref=rq_send.at[2],
-                dst_ref=rq_recv.at[N_GRP + j],
-                send_sem=rq_ssem.at[N_GRP + j],
-                recv_sem=rq_rsem.at[N_GRP + j],
-                device_id=target,
-                device_id_type=MESH,
-            )
-        )
-    for copy in halo_requests:
-        copy.start()
-    loads["flag"].wait()
 
     for q in range(QUANT):
         x = jnp.where(ids == 0, lev[0, q], jnp.where(ids == 1, lev[1, q], lev[2, q]))

time: 40.6 us -> 39.3 us (0.968)
  Pallas kernels: 39.7 us -> 38.4 us
    pallas_call x1, Pallas kernels: 39.7 us -> 38.4 us  [on_device(): pl.pallas_call(kernel, out_shape=jax.ShapeDtypeStruct((QUANT, MODES, ELEM...]
where the time goes in v3:
time: 39.3 us; the launch traced here: 39.1 us
  Pallas kernels  38.4 us (98%)
  local copies, waits for them, and re-layouts  0.7 us (2%)
    pallas_call x1, Pallas kernels, on_device(): pl.pallas_call(kernel, out_shape=jax.ShapeDtypeStruct((QUANT, MODES, ELEM...  38.4 us

profile of v3, /device:TPU:1, one launch (start us, length us, event | category | flops | bytes accessed | tf_op | source)
XLA Modules:
  0.0 39.1 jit_solution(10702063959325762126)
XLA Ops:
  0.0 38.4 %shard_map.127 = f32[9,56,128]{2,1,0:T(8,128)S(1)} custom-call(f32[9,56,128]{2,1,0:T(8,128)} %old_h.1, f32[3,56,56]{2,1,0:T(8,128)} %stiff_h.1, f32[9,9,3,128]{3,2,1,0:T(4,128)} %bitcast.7, f32[4,56,56]{2,1,0:T(8,128)} %lown_h.1, f32[4,4,56,56]{3,2,1,0:T(8,128)} %lacross_h.1, f32[2,9,9,4,128]{4,3,2,1,0:T(4,128)} %bitcast.6, s32[1,128]{1,0:T(1,128)} %bitcast.8, ...), custom_call_target="tpu_custom_call" | custom-call | tf_op jit(solution)/shard_map/pallas_call | solution.py:612
  38.4 0.7 %copy.15 = f32[9,56,128]{2,1,0:T(8,128)} copy(f32[9,56,128]{2,1,0:T(8,128)S(1)} %shard_map.127) | data formatting | bytes 516096
